TPU v7x, 32 devices: a whole 2x2x4 slice. The times are simulated.
32 devices in a mesh: freq: 4 (over y, x), row: 8 (over z, core).
Axes of the slice: x: 2, y: 2, z: 4, core: 2. Of those that a mesh axis runs over, the one named last changes fastest.
Arguments:
- data: bfloat16 [4, 2, 2048, 2048], P('freq', None, 'row'), may hold values from -60 to 60
Outputs:
- solution: float32 [4, 2, 2048, 2048], P('freq', None, 'row')
- direction: float32 [4, 2, 2048, 2048], P('freq', None, 'row')
All inputs are finite; a program needn't handle non-finite values.
Results may differ from a plain program's by a relative error of at most 0.0042.
Values may be sent and summed in bfloat16 or wider, within the bound.
A program may use at most 128 MiB of HBM per device.

v0:
```python
import jax
import jax.numpy as jnp
from jax import lax
from jax.sharding import PartitionSpec as P

ITERS = 2


def times_data(rounded, block):
    real_part = jnp.einsum(
        "frk,fkn->frn", rounded[:, 0], block[:, 0], preferred_element_type=jnp.float32
    ) - jnp.einsum("frk,fkn->frn", rounded[:, 1], block[:, 1], preferred_element_type=jnp.float32)
    imag_part = jnp.einsum(
        "frk,fkn->frn", rounded[:, 0], block[:, 1], preferred_element_type=jnp.float32
    ) + jnp.einsum("frk,fkn->frn", rounded[:, 1], block[:, 0], preferred_element_type=jnp.float32)
    return jnp.stack([real_part, imag_part], axis=1)


def times_adjoint(rounded, block):
    real_part = jnp.einsum(
        "frk,fnk->frn", rounded[:, 0], block[:, 0], preferred_element_type=jnp.float32
    ) + jnp.einsum("frk,fnk->frn", rounded[:, 1], block[:, 1], preferred_element_type=jnp.float32)
    imag_part = jnp.einsum(
        "frk,fnk->frn", rounded[:, 1], block[:, 0], preferred_element_type=jnp.float32
    ) - jnp.einsum("frk,fnk->frn", rounded[:, 0], block[:, 1], preferred_element_type=jnp.float32)
    return jnp.stack([real_part, imag_part], axis=1)


def on_device(data):
    order = data.shape[3]
    weight = 1.0 / (3.0 * (2.0 * order) ** 0.5)
    observed = data.astype(jnp.float32)
    zeros = jnp.zeros_like(observed)
    whole = lax.all_gather(data, "row", axis=2, tiled=True)
    first_image = observed - weight * times_adjoint(observed.astype(jnp.bfloat16), whole)

    def pair_step(data_raw, model_unit, image):
        data_sq, image_sq, cross, model_sq = lax.psum(
            (
                jnp.sum(data_raw * data_raw),
                jnp.sum(image * image),
                jnp.sum(image * model_unit),
                jnp.sum(model_unit * model_unit),
            ),
            ("freq", "row"),
        )
        beta_now = jnp.sqrt(data_sq)
        model_raw = image / beta_now - beta_now * model_unit
        alpha_now = jnp.sqrt(
            image_sq / (beta_now * beta_now) - 2.0 * cross + beta_now * beta_now * model_sq
        )
        return (beta_now, data_raw / beta_now, model_raw, alpha_now, model_raw / alpha_now)

    beta_now, data_unit, model_raw, alpha_now, model_unit = pair_step(observed, zeros, first_image)
    solution = zeros
    direction = model_unit
    phi_bar = beta_now
    rho_bar = alpha_now
    for iteration in range(ITERS):
        data_raw = (
            model_raw - weight * times_data(model_raw.astype(jnp.bfloat16), whole)
        ) / alpha_now - alpha_now * data_unit
        beta_now, data_unit, model_raw, alpha_now, model_unit = pair_step(
            data_raw,
            model_unit,
            data_raw - weight * times_adjoint(data_raw.astype(jnp.bfloat16), whole),
        )
        rho_value = jnp.sqrt(rho_bar * rho_bar + beta_now * beta_now)
        cosine = rho_bar / rho_value
        sine_value = beta_now / rho_value
        theta_value = sine_value * alpha_now
        rho_bar = -cosine * alpha_now
        phi_value = cosine * phi_bar
        phi_bar = sine_value * phi_bar
        solution = solution + phi_value / rho_value * direction
        direction = model_unit - theta_value / rho_value * direction
    return (solution, direction)


def solution(mesh):
    return jax.shard_map(
        on_device,
        mesh=mesh,
        in_specs=(P("freq", None, "row", None),),
        out_specs=(P("freq", None, "row", None), P("freq", None, "row", None)),
        check_vma=False,
    )
```

profile of v0, /device:TPU:0, one launch (start us, length us, event | category | flops | bytes accessed | tf_op | source)
XLA Modules:
  0.0 440.0 jit_solution(2059661497259600702)
XLA Ops:
  7.9 155.5 %all-gather.2.cloned.1.call-done = bf16[1,2,2048,2048]{3,2,1,0:T(8,128)(2,1)} async-done(((bf16[1,2,256,2048]{3,2,1,0:T(8,128)(2,1)}), bf16[1,2,2048,2048]{3,2,1,0:T(8,128)(2,1)}) %all-gather.2.cloned.1.call-update) | async-done | bytes 16777232 | tf_op jit(solution)/shard_map/all_gather | solution.py:34
  163.4 6.2 %fusion.20 = f32[256,2048]{1,0:T(8,128)S(1)} fusion(bf16[1,2,256,2048]{3,2,1,0:T(8,128)(2,1)} %param.1, bf16[1,2,2048,2048]{3,2,1,0:T(8,128)(2,1)} %all-gather.2.cloned.1.call-done), kind=kOutput, calls=%fused_computation.65 | convolution fusion | flops 2147483648 | bytes 11534336 | tf_op jit(solution)/shard_map/frk,fnk->frn/dot_general | solution.py:23
  169.7 5.9 %fusion.24 = f32[256,2048]{1,0:T(8,128)S(1)} fusion(bf16[1,2,256,2048]{3,2,1,0:T(8,128)(2,1)S(1)} %copy-done.3, bf16[1,2,2048,2048]{3,2,1,0:T(8,128)(2,1)} %all-gather.2.cloned.1.call-done), kind=kOutput, calls=%fused_computation.69 | convolution fusion | flops 2147483648 | bytes 11534336 | tf_op jit(solution)/shard_map/frk,fnk->frn/dot_general | solution.py:20
  175.6 2.4 fusion.18
  178.0 2.4 fusion.19
  180.4 1.9 multiply_reduce_fusion.8
  182.3 39.7 %all-reduce.2 = (f32[]{:T(128)}, f32[]{:T(128)}, f32[]{:T(128)}, f32[]{:T(128)}) all-reduce(f32[]{:T(128)} %get-tuple-element.7, f32[]{:T(128)} %get-tuple-element.12, f32[]{:T(128)} %get-tuple-element.6, f32[]{:T(128)} %constant.2.clone.1), channel_id=1, replica_groups=mesh['freq'=4,'row'=8] {'freq','row'}, use_global_device_ids=true, to_apply=%region_1.0 | all-reduce | flops 4 | bytes 32 | tf_op jit(solution)/shard_map/psum | solution.py:38
  224.6 4.4 %fusion.38 = bf16[1,2,256,2048]{3,2,1,0:T(8,128)(2,1)} fusion(f32[]{:T(128)S(6)} %mul.197, f32[]{:T(128)S(6)} %sqrt.24, f32[1,1,256,2048]{3,2,1,0:T(8,128)} %copy-done.5, f32[1,1,256,2048]{3,2,1,0:T(8,128)} %copy-done.7, bf16[1,2,256,2048]{3,2,1,0:T(8,128)(2,1)S(1)} %copy-done.3), kind=kLoop, calls=%fused_computation.83 | loop fusion | flops 7340032 | bytes 8388616 | tf_op jit(solution)/shard_map/convert_element_type | solution.py:61
  229.0 6.2 %fusion.26 = f32[256,2048]{1,0:T(8,128)S(1)} fusion(bf16[1,2,256,2048]{3,2,1,0:T(8,128)(2,1)} %fusion.38, bf16[1,2,2048,2048]{3,2,1,0:T(8,128)(2,1)} %all-gather.2.cloned.1.call-done), kind=kOutput, calls=%fused_computation.71 | convolution fusion | flops 2147483648 | bytes 11534336 | tf_op jit(solution)/shard_map/frk,fkn->frn/dot_general | solution.py:13
  235.2 5.7 %fusion.27 = f32[256,2048]{1,0:T(8,128)S(1)} fusion(bf16[1,2,256,2048]{3,2,1,0:T(8,128)(2,1)S(1)} %copy-done.12, bf16[1,2,2048,2048]{3,2,1,0:T(8,128)(2,1)} %all-gather.2.cloned.1.call-done), kind=kOutput, calls=%fused_computation.72 | convolution fusion | flops 2147483648 | bytes 11534336 | tf_op jit(solution)/shard_map/frk,fkn->frn/dot_general | solution.py:10
  240.9 5.8 %fusion.16 = f32[1,1,256,2048]{3,2,1,0:T(8,128)S(1)} fusion(f32[256,2048]{1,0:T(8,128)S(1)} %fusion.26, bf16[1,2,256,2048]{3,2,1,0:T(8,128)(2,1)S(1)} %copy-done.12, bf16[1,2,2048,2048]{3,2,1,0:T(8,128)(2,1)} %all-gather.2.cloned.1.call-done), kind=kOutput, calls=%fused_computation.48 | convolution fusion | flops 2148007936 | bytes 13631488 | tf_op jit(solution)/shard_map/frk,fkn->frn/dot_general | solution.py:15
  246.8 5.9 %fusion.17 = f32[1,1,256,2048]{3,2,1,0:T(8,128)S(1)} fusion(f32[256,2048]{1,0:T(8,128)S(1)} %fusion.27, bf16[1,2,256,2048]{3,2,1,0:T(8,128)(2,1)S(1)} %copy-done.12, bf16[1,2,2048,2048]{3,2,1,0:T(8,128)(2,1)} %all-gather.2.cloned.1.call-done), kind=kOutput, calls=%fused_computation.50 | convolution fusion | flops 2148007936 | bytes 13631488 | tf_op jit(solution)/shard_map/frk,fkn->frn/dot_general | solution.py:12
  252.7 1.8 fusion.42
  254.6 7.3 %fusion.29 = f32[256,2048]{1,0:T(8,128)S(1)} fusion(bf16[1,2,256,2048]{3,2,1,0:T(8,128)(2,1)S(1)} %get-tuple-element.30, bf16[1,2,2048,2048]{3,2,1,0:T(8,128)(2,1)} %all-gather.2.cloned.1.call-done), kind=kOutput, calls=%fused_computation.74 | convolution fusion | flops 2147483648 | bytes 11534336 | tf_op jit(solution)/shard_map/frk,fnk->frn/dot_general | solution.py:23
  261.8 5.7 %fusion.28 = f32[256,2048]{1,0:T(8,128)S(1)} fusion(bf16[1,2,256,2048]{3,2,1,0:T(8,128)(2,1)S(1)} %get-tuple-element.30, bf16[1,2,2048,2048]{3,2,1,0:T(8,128)(2,1)} %all-gather.2.cloned.1.call-done), kind=kOutput, calls=%fused_computation.73 | convolution fusion | flops 2147483648 | bytes 11534336 | tf_op jit(solution)/shard_map/frk,fnk->frn/dot_general | solution.py:20
  267.6 5.7 %fusion.14 = f32[1,1,256,2048]{3,2,1,0:T(8,128)S(1)} fusion(f32[256,2048]{1,0:T(8,128)S(1)} %fusion.29, bf16[1,2,256,2048]{3,2,1,0:T(8,128)(2,1)S(1)} %get-tuple-element.30, bf16[1,2,2048,2048]{3,2,1,0:T(8,128)(2,1)} %all-gather.2.cloned.1.call-done), kind=kOutput, calls=%fused_computation.44 | convolution fusion | flops 2148007936 | bytes 13631488 | tf_op jit(solution)/shard_map/frk,fnk->frn/dot_general | solution.py:25
  273.4 6.5 %fusion.15 = f32[1,1,256,2048]{3,2,1,0:T(8,128)S(1)} fusion(f32[256,2048]{1,0:T(8,128)S(1)} %fusion.28, bf16[1,2,256,2048]{3,2,1,0:T(8,128)(2,1)S(1)} %get-tuple-element.30, bf16[1,2,2048,2048]{3,2,1,0:T(8,128)(2,1)} %all-gather.2.cloned.1.call-done), kind=kOutput, calls=%fused_computation.46 | convolution fusion | flops 2148007936 | bytes 13631488 | tf_op jit(solution)/shard_map/frk,fnk->frn/dot_general | solution.py:22
  279.9 4.2 multiply_reduce_fusion.5
  284.1 41.6 %all-reduce.1 = (f32[]{:T(128)}, f32[]{:T(128)}, f32[]{:T(128)}, f32[]{:T(128)}) all-reduce(f32[]{:T(128)} %get-tuple-element.11, f32[]{:T(128)} %get-tuple-element.5, f32[]{:T(128)} %get-tuple-element.4, f32[]{:T(128)} %get-tuple-element.10), channel_id=1, replica_groups=mesh['freq'=4,'row'=8] {'freq','row'}, use_global_device_ids=true, to_apply=%region_8.0 | all-reduce | flops 4 | bytes 32 | tf_op jit(solution)/shard_map/psum | solution.py:38
  328.4 5.5 %fusion.41 = (bf16[1,2,256,2048]{3,2,1,0:T(8,128)(2,1)S(1)}, f32[1,2,256,2048]{3,2,1,0:T(8,128)S(1)}) fusion(f32[1,2,256,2048]{3,2,1,0:T(8,128)} %get-tuple-element.29, f32[]{:T(128)S(6)} %sqrt.26, f32[1,2,256,2048]{3,2,1,0:T(8,128)} %copy-done, f32[1,1,256,2048]{3,2,1,0:T(8,128)} %copy-done.10, f32[1,1,256,2048]{3,2,1,0:T(8,128)} %copy-done.11), kind=kLoop, calls=%fused_computation.85 | loop fusion | flops 7340032 | bytes 18874372 | tf_op jit(solution)/shard_map/convert_element_type | solution.py:61
  333.9 8.1 %fusion.30 = f32[256,2048]{1,0:T(8,128)S(1)} fusion(bf16[1,2,256,2048]{3,2,1,0:T(8,128)(2,1)S(1)} %get-tuple-element.27, bf16[1,2,2048,2048]{3,2,1,0:T(8,128)(2,1)} %all-gather.2.cloned.1.call-done), kind=kOutput, calls=%fused_computation.75 | convolution fusion | flops 2147483648 | bytes 11534336 | tf_op jit(solution)/shard_map/frk,fkn->frn/dot_general | solution.py:13
  342.0 2.3 fusion.31
  344.4 2.4 fusion.12
  346.8 5.9 %fusion.13 = f32[1,1,256,2048]{3,2,1,0:T(8,128)S(1)} fusion(f32[256,2048]{1,0:T(8,128)S(1)} %fusion.31, bf16[1,2,256,2048]{3,2,1,0:T(8,128)(2,1)S(1)} %get-tuple-element.27, bf16[1,2,2048,2048]{3,2,1,0:T(8,128)(2,1)} %all-gather.2.cloned.1.call-done), kind=kOutput, calls=%fused_computation.42 | convolution fusion | flops 2148007936 | bytes 13631488 | tf_op jit(solution)/shard_map/frk,fkn->frn/dot_general | solution.py:12
  352.7 1.7 fusion.39
  354.5 7.3 %fusion.33 = f32[256,2048]{1,0:T(8,128)S(1)} fusion(bf16[1,2,256,2048]{3,2,1,0:T(8,128)(2,1)S(1)} %get-tuple-element.25, bf16[1,2,2048,2048]{3,2,1,0:T(8,128)(2,1)} %all-gather.2.cloned.1.call-done), kind=kOutput, calls=%fused_computation.78 | convolution fusion | flops 2147483648 | bytes 11534336 | tf_op jit(solution)/shard_map/frk,fnk->frn/dot_general | solution.py:23
  361.7 5.7 %fusion.32 = f32[256,2048]{1,0:T(8,128)S(1)} fusion(bf16[1,2,256,2048]{3,2,1,0:T(8,128)(2,1)S(1)} %get-tuple-element.25, bf16[1,2,2048,2048]{3,2,1,0:T(8,128)(2,1)} %all-gather.2.cloned.1.call-done), kind=kOutput, calls=%fused_computation.77 | convolution fusion | flops 2147483648 | bytes 11534336 | tf_op jit(solution)/shard_map/frk,fnk->frn/dot_general | solution.py:20
  367.5 5.7 %fusion.10 = f32[1,1,256,2048]{3,2,1,0:T(8,128)S(1)} fusion(f32[256,2048]{1,0:T(8,128)S(1)} %fusion.33, bf16[1,2,256,2048]{3,2,1,0:T(8,128)(2,1)S(1)} %get-tuple-element.25, bf16[1,2,2048,2048]{3,2,1,0:T(8,128)(2,1)} %all-gather.2.cloned.1.call-done), kind=kOutput, calls=%fused_computation.36 | convolution fusion | flops 2148007936 | bytes 13631488 | tf_op jit(solution)/shard_map/frk,fnk->frn/dot_general | solution.py:25
  373.2 5.7 %fusion.11 = f32[1,1,256,2048]{3,2,1,0:T(8,128)S(1)} fusion(f32[256,2048]{1,0:T(8,128)S(1)} %fusion.32, bf16[1,2,256,2048]{3,2,1,0:T(8,128)(2,1)S(1)} %get-tuple-element.25, bf16[1,2,2048,2048]{3,2,1,0:T(8,128)(2,1)} %all-gather.2.cloned.1.call-done), kind=kOutput, calls=%fused_computation.38 | convolution fusion | flops 2148007936 | bytes 13631488 | tf_op jit(solution)/shard_map/frk,fnk->frn/dot_general | solution.py:22
  379.0 2.2 multiply_reduce_fusion.1
  381.2 39.8 %all-reduce = (f32[]{:T(128)}, f32[]{:T(128)}, f32[]{:T(128)}, f32[]{:T(128)}) all-reduce(f32[]{:T(128)} %get-tuple-element.9, f32[]{:T(128)} %get-tuple-element.3, f32[]{:T(128)} %get-tuple-element.2, f32[]{:T(128)} %get-tuple-element.8), channel_id=1, replica_groups=mesh['freq'=4,'row'=8] {'freq','row'}, use_global_device_ids=true, to_apply=%region_16.0 | all-reduce | flops 4 | bytes 32 | tf_op jit(solution)/shard_map/psum | solution.py:38
  424.0 8.7 %multiply_subtract_fusion = (f32[1,2,256,2048]{3,2,1,0:T(8,128)}, f32[1,2,256,2048]{3,2,1,0:T(8,128)}) fusion(f32[1,2,256,2048]{3,2,1,0:T(8,128)} %get-tuple-element.29, f32[]{:T(128)S(6)} %div.111, f32[]{:T(128)S(6)} %sqrt.31, f32[]{:T(128)S(6)} %sqrt.29, f32[]{:T(128)S(6)} %div.104, f32[1,2,256,2048]{3,2,1,0:T(8,128)} %copy-done.4, ...), kind=kLoop, calls=%fused_computation.20 | loop fusion | flops 15728640 | bytes 25165852 | tf_op jit(solution)/shard_map/sub | solution.py:76
  (46 shorter events, 0.8 us)
Async XLA Ops:
  7.2 156.3 %all-gather.2.cloned.1.call-start = ((), (), s32[]{:S(2)}) async-start(), calls=%async_computation | async-start | bytes 18874368 | tf_op jit(solution)/shard_map/all_gather | solution.py:34
  7.9 161.7 %copy-start.3 = (bf16[1,2,256,2048]{3,2,1,0:T(8,128)(2,1)S(1)}, bf16[1,2,256,2048]{3,2,1,0:T(8,128)(2,1)}, u32[]{:S(2)}) copy-start(bf16[1,2,256,2048]{3,2,1,0:T(8,128)(2,1)} %param.1) | copy-start | bytes 6291460
  163.4 12.2 %slice-start = ((s8[16777216]{0:T(1024)(128)(4,1)}), s8[4194304]{0:T(1024)(128)(4,1)S(1)}, s32[]{:S(2)}) async-start(s8[16777216]{0:T(1024)(128)(4,1)} %bitcast.86), calls=%async_computation.1 | async-start | bytes 8388608
  163.4 12.2 %slice-start.1 = ((s8[16777216]{0:T(1024)(128)(4,1)}), s8[4194304]{0:T(1024)(128)(4,1)S(1)}, s32[]{:S(2)}) async-start(s8[16777216]{0:T(1024)(128)(4,1)} %bitcast.86), calls=%async_computation.2 | async-start | bytes 8388608
  169.6 5.9 %slice-start.2 = ((s8[16777216]{0:T(1024)(128)(4,1)}), s8[4194304]{0:T(1024)(128)(4,1)S(1)}, s32[]{:S(2)}) async-start(s8[16777216]{0:T(1024)(128)(4,1)} %bitcast.86), calls=%async_computation.3 | async-start | bytes 8388608
  169.7 5.9 %slice-start.3 = ((s8[16777216]{0:T(1024)(128)(4,1)}), s8[4194304]{0:T(1024)(128)(4,1)S(1)}, s32[]{:S(2)}) async-start(s8[16777216]{0:T(1024)(128)(4,1)} %bitcast.86), calls=%async_computation.4 | async-start | bytes 8388608
  178.0 2.4 copy-start.5
  180.4 1.9 copy-start.7
  229.0 6.2 %copy-start.12 = (bf16[1,2,256,2048]{3,2,1,0:T(8,128)(2,1)S(1)}, bf16[1,2,256,2048]{3,2,1,0:T(8,128)(2,1)}, u32[]{:S(2)}) copy-start(bf16[1,2,256,2048]{3,2,1,0:T(8,128)(2,1)} %fusion.38) | copy-start | bytes 6291460
  246.7 6.0 %copy-start.6 = (f32[1,1,256,2048]{3,2,1,0:T(8,128)S(1)}, f32[1,1,256,2048]{3,2,1,0:T(8,128)}, u32[]{:S(2)}) copy-start(f32[1,1,256,2048]{3,2,1,0:T(8,128)} %copy-done.5) | copy-start | bytes 6291460
  246.7 6.0 %copy-start.8 = (f32[1,1,256,2048]{3,2,1,0:T(8,128)S(1)}, f32[1,1,256,2048]{3,2,1,0:T(8,128)}, u32[]{:S(2)}) copy-start(f32[1,1,256,2048]{3,2,1,0:T(8,128)} %copy-done.7) | copy-start | bytes 6291460
  254.6 25.3 %copy-start = (f32[1,2,256,2048]{3,2,1,0:T(8,128)}, f32[1,2,256,2048]{3,2,1,0:T(8,128)S(1)}, u32[]{:S(2)}) copy-start(f32[1,2,256,2048]{3,2,1,0:T(8,128)S(1)} %get-tuple-element.31) | copy-start | bytes 12582916
  273.4 6.5 %copy-start.10 = (f32[1,1,256,2048]{3,2,1,0:T(8,128)}, f32[1,1,256,2048]{3,2,1,0:T(8,128)S(1)}, u32[]{:S(2)}) copy-start(f32[1,1,256,2048]{3,2,1,0:T(8,128)S(1)} %fusion.14) | copy-start | bytes 6291460
  279.9 4.3 copy-start.11
  328.4 13.6 %slice-start.4 = ((s8[16777216]{0:T(1024)(128)(4,1)}), s8[4194304]{0:T(1024)(128)(4,1)S(1)}, s32[]{:S(2)}) async-start(s8[16777216]{0:T(1024)(128)(4,1)} %bitcast.88), calls=%async_computation.5 | async-start | bytes 8388608
  328.4 13.6 %slice-start.5 = ((s8[16777216]{0:T(1024)(128)(4,1)}), s8[4194304]{0:T(1024)(128)(4,1)S(1)}, s32[]{:S(2)}) async-start(s8[16777216]{0:T(1024)(128)(4,1)} %bitcast.88), calls=%async_computation.6 | async-start | bytes 8388608
  328.4 13.6 %slice-start.6 = ((s8[16777216]{0:T(1024)(128)(4,1)}), s8[4194304]{0:T(1024)(128)(4,1)S(1)}, s32[]{:S(2)}) async-start(s8[16777216]{0:T(1024)(128)(4,1)} %bitcast.88), calls=%async_computation.7 | async-start | bytes 8388608
  333.9 45.1 %copy-start.2 = (f32[1,2,256,2048]{3,2,1,0:T(8,128)}, f32[1,2,256,2048]{3,2,1,0:T(8,128)S(1)}, u32[]{:S(2)}) copy-start(f32[1,2,256,2048]{3,2,1,0:T(8,128)S(1)} %get-tuple-element.28) | copy-start | bytes 12582916
  333.9 8.1 %slice-start.7 = ((s8[16777216]{0:T(1024)(128)(4,1)}), s8[4194304]{0:T(1024)(128)(4,1)S(1)}, s32[]{:S(2)}) async-start(s8[16777216]{0:T(1024)(128)(4,1)} %bitcast.88), calls=%async_computation.8 | async-start | bytes 8388608
  346.8 5.9 %copy-start.1 = (f32[1,2,256,2048]{3,2,1,0:T(8,128)S(1)}, f32[1,2,256,2048]{3,2,1,0:T(8,128)}, u32[]{:S(2)}) copy-start(f32[1,2,256,2048]{3,2,1,0:T(8,128)} %copy-done) | copy-start | bytes 12582916
  354.4 24.6 %copy-start.4 = (f32[1,2,256,2048]{3,2,1,0:T(8,128)}, f32[1,2,256,2048]{3,2,1,0:T(8,128)S(1)}, u32[]{:S(2)}) copy-start(f32[1,2,256,2048]{3,2,1,0:T(8,128)S(1)} %get-tuple-element.26) | copy-start | bytes 12582916
  379.0 2.2 copy-start.9
Sparse Core Ops, SparseCore 0:
  9.6 153.7 all-gather.1
where the time goes:
time: 448 us; the launch traced here: 440 us
  waiting for transfers between devices  156 us (35%)
  blocking collectives  121 us (27%)
  matrix products  109 us (24%)
  other arithmetic  30.6 us (7%)
  between operations  23.1 us (5%)
    all_gather x1, waiting for transfers between devices, on_device(): whole = lax.all_gather(data, 'row', axis=2, tiled=True)  156 us
    psum x3, blocking collectives, pair_step(): lax.psum((jnp.sum(data_raw * data_raw), jnp.sum(image * image), jnp.sum(i...  121 us
    dot_general x3, matrix products, times_adjoint(): jnp.einsum('frk,fnk->frn', rounded[:, 1], block[:, 0], preferred_element_...  20.7 us
    dot_general x3, matrix products, times_adjoint(): jnp.einsum('frk,fnk->frn', rounded[:, 0], block[:, 0], preferred_element_...  17.4 us
    dot_general x3, matrix products, times_adjoint(): jnp.einsum('frk,fnk->frn', rounded[:, 1], block[:, 1], preferred_element_...  14.6 us
    dot_general x2, matrix products, times_data(): jnp.einsum('frk,fkn->frn', rounded[:, 0], block[:, 1], preferred_element_...  14.2 us
    dot_general x3, matrix products, times_adjoint(): jnp.einsum('frk,fnk->frn', rounded[:, 0], block[:, 1], preferred_element_...  13.9 us
    dot_general x2, matrix products, times_data(): jnp.einsum('frk,fkn->frn', rounded[:, 1], block[:, 1], preferred_element_...  11.8 us
  transfers between devices with their start and end apart: 1, of which 1 were waited for; matrix products, arithmetic and copies ran while one was open for 0% of the time, Pallas kernels for 0%

commit v1 on v0

v1 whole, which is shorter than its diff:
```python
import functools

import jax
import jax.numpy as jnp
from jax import lax
from jax.experimental import pallas as pl
from jax.experimental.pallas import tpu as pltpu
from jax.sharding import PartitionSpec as P

ITERS = 2
MESH = pl.DeviceIdType.MESH
F32 = jnp.float32
BF16 = jnp.bfloat16


def dot(a, b):
    return lax.dot_general(a, b, (((1,), (0,)), ((), ())), preferred_element_type=F32)


def dot_t(a, b):
    return lax.dot_general(a, b, (((1,), (1,)), ((), ())), preferred_element_type=F32)


def lane_sums(x):
    s = jnp.sum(x, axis=0, keepdims=True)
    return functools.reduce(jnp.add, [s[:, i : i + 128] for i in range(0, s.shape[1], 128)])


def kernel(
    n, nf, weight, data, sol_out, dir_out,
    full, va, vd, d_raw, m_raw, image, direc, work, stats, slots, sums, fslots,
    load_sem, ssem, rsem, st_s, st_r, sf_s, sf_r, out_sem,
):
    rows, order = data.shape[2], data.shape[3]
    m = n // 2
    me = lax.axis_index("row")
    mf = lax.axis_index("freq")
    z, c = lax.div(me, 2), lax.rem(me, 2)
    overlap = rows % 128 == 0
    unit = rows if overlap else min(order, 256)
    wide = min(order, 512)

    def at_row(r):
        return {"row": r}

    def piece(zb, cc, p):
        start = pl.multiple_of((zb * 2 + cc) * rows, rows)
        return full.at[p, pl.ds(start, rows), :]

    loads = []
    for p in range(2):
        loads.append(pltpu.make_async_copy(data.at[0, p], piece(z, c, p), load_sem.at[p]))
        loads.append(
            pltpu.make_async_copy(
                data.at[0, p], vd.at[pl.ds(p * rows, rows), :], load_sem.at[2 + p]
            )
        )
    for copy in loads:
        copy.start()

    barrier = pltpu.get_barrier_semaphore()

    @pl.loop(1, n)
    def _(k):
        pl.semaphore_signal(
            barrier, inc=1, device_id=at_row(lax.rem(me + k, n)), device_id_type=MESH
        )

    @pl.loop(1, nf)
    def _(k):
        pl.semaphore_signal(
            barrier, inc=1, device_id={"freq": lax.rem(mf + k, nf)}, device_id_type=MESH
        )

    for copy in loads:
        copy.wait()

    stats[...] = jnp.zeros_like(stats)

    @pl.loop(0, order // wide)
    def _(i):
        x = vd[:, pl.ds(pl.multiple_of(i * wide, wide), wide)].astype(F32)
        stats[0, 0:1, :] += lane_sums(x * x)

    pl.semaphore_wait(barrier, n - 1 + nf - 1)

    def row_stat(k, j):
        return pltpu.make_async_remote_copy(
            src_ref=stats.at[k], dst_ref=slots.at[k, me], send_sem=st_s.at[k, j],
            recv_sem=st_r.at[k, me], device_id=at_row(j), device_id_type=MESH,
        )

    def row_arrival(k, j):
        return pltpu.make_async_remote_copy(
            src_ref=stats.at[k], dst_ref=slots.at[k, j], send_sem=st_s.at[k, j],
            recv_sem=st_r.at[k, j], device_id=at_row(j), device_id_type=MESH,
        )

    def freq_stat(k, j):
        return pltpu.make_async_remote_copy(
            src_ref=sums.at[k], dst_ref=fslots.at[k, mf], send_sem=sf_s.at[k, j],
            recv_sem=sf_r.at[k, mf], device_id={"freq": j}, device_id_type=MESH,
        )

    def freq_arrival(k, j):
        return pltpu.make_async_remote_copy(
            src_ref=sums.at[k], dst_ref=fslots.at[k, j], send_sem=sf_s.at[k, j],
            recv_sem=sf_r.at[k, j], device_id={"freq": j}, device_id_type=MESH,
        )

    def start_sum(k):
        slots[k, me] = stats[k]

        @pl.loop(1, n)
        def _(i):
            row_stat(k, lax.rem(me + i, n)).start()

    def finish_sum(k):
        @pl.loop(1, n)
        def _(i):
            row_arrival(k, lax.rem(me + i, n)).wait_recv()

        total = lax.fori_loop(
            1, n, lambda j, t: t + slots[k, j], slots[k, 0]
        )
        sums[k] = total
        fslots[k, mf] = total

        @pl.loop(1, nf)
        def _(i):
            freq_stat(k, lax.rem(mf + i, nf)).start()

        @pl.loop(1, nf)
        def _(i):
            freq_arrival(k, lax.rem(mf + i, nf)).wait_recv()

        total = lax.fori_loop(
            1, nf, lambda j, t: t + fslots[k, j], fslots[k, 0]
        )
        values = jnp.sum(total, axis=1, keepdims=True)
        return [values[q : q + 1, :] for q in range(4)]

    def drain_sum(k):
        @pl.loop(1, n)
        def _(i):
            row_stat(k, lax.rem(me + i, n)).wait_send()

        @pl.loop(1, nf)
        def _(i):
            freq_stat(k, lax.rem(mf + i, nf)).wait_send()

    def block_copy(lane, zb, cc, p, target):
        return pltpu.make_async_remote_copy(
            src_ref=piece(zb, cc, p), dst_ref=piece(zb, cc, p),
            send_sem=ssem.at[lane, zb, p], recv_sem=rsem.at[zb * 2 + cc, p],
            device_id=at_row(target), device_id_type=MESH,
        )

    sibling = z * 2 + (1 - c)

    def spread(zb, p, below, above):
        @pl.when(below & (z + 1 < m))
        def _():
            block_copy(0, zb, c, p, lax.rem(me + 2, n)).start()

        @pl.when(above & (z > 0))
        def _():
            block_copy(1, zb, c, p, lax.rem(me + n - 2, n)).start()

        block_copy(2, zb, c, p, sibling).start()

    def settle(zb, p):
        @pl.when((zb <= z) & (z + 1 < m))
        def _():
            block_copy(0, zb, c, p, lax.rem(me + 2, n)).wait_send()

        @pl.when((zb >= z) & (z > 0))
        def _():
            block_copy(1, zb, c, p, lax.rem(me + n - 2, n)).wait_send()

        block_copy(2, zb, c, p, sibling).wait_send()

    start_sum(0)
    yes = m > 0
    for p in range(2):
        spread(z, p, jnp.bool_(yes), jnp.bool_(yes))

    @pl.loop(0, order // wide)
    def _(i):
        cols = pl.ds(pl.multiple_of(i * wide, wide), wide)
        work[:, cols] = jnp.zeros((2 * rows, wide), F32)

    beta = jnp.sqrt(finish_sum(0)[0])

    def process(start):
        band = pl.ds(pl.multiple_of(start, unit), unit)
        tr = dot_t(vd[...], full[0, band, :])
        ti = dot_t(vd[...], full[1, band, :])
        fit = jnp.concatenate([tr[:rows] + ti[rows:], tr[rows:] - ti[:rows]], axis=0)
        raw = (vd[:, band].astype(F32) - weight * fit) / beta
        m_raw[:, band] = raw
        stats[1, 0:1, :] += lane_sums(raw * raw)
        va[:, band] = raw.astype(BF16)

        @pl.loop(0, order // wide)
        def _(i):
            cols = pl.ds(pl.multiple_of(i * wide, wide), wide)
            v = va[:, band]
            a = dot(v, full[0, band, cols])
            b = dot(v, full[1, band, cols])
            work[:, cols] += jnp.concatenate(
                [a[:rows] - b[rows:], a[rows:] + b[:rows]], axis=0
            )

    @pl.loop(0, m)
    def _(s):
        @pl.when(s > 0)
        def _():
            for p in range(2):
                @pl.when(z - s >= 0)
                def _():
                    block_copy(0, z - s, c, p, sibling).wait_recv()
                    spread(z - s, p, jnp.bool_(True), jnp.bool_(False))

                @pl.when(z + s < m)
                def _():
                    block_copy(0, z + s, c, p, sibling).wait_recv()
                    spread(z + s, p, jnp.bool_(False), jnp.bool_(True))

        @pl.loop(0, 4)
        def _(t):
            up = lax.div(t, 2)
            other = lax.rem(t, 2)
            zb = z - s + 2 * s * up
            cc = c + other * (1 - 2 * c)

            @pl.when((zb >= 0) & (zb < m) & ((s > 0) | (t < 2)))
            def _():
                @pl.when(other == 1)
                def _():
                    for p in range(2):
                        block_copy(0, zb, cc, p, sibling).wait_recv()

                if overlap:
                    process((zb * 2 + cc) * rows)

    if not overlap:
        @pl.loop(0, order // unit)
        def _(u):
            process(u * unit)

    start_sum(1)
    alpha = jnp.sqrt(finish_sum(1)[0])

    chunk = min(order, 256)
    phi_bar, rho_bar = beta, alpha
    for it in range(ITERS):
        k = 2 + it
        inv_alpha, keep = 1.0 / alpha, alpha / beta

        @pl.loop(0, order // wide)
        def _(i):
            cols = pl.ds(pl.multiple_of(i * wide, wide), wide)
            if it == 0:
                fit = work[:, cols]
                old = vd[:, cols].astype(F32)
            else:
                a = dot(va[...], full[0, :, cols])
                b = dot(va[...], full[1, :, cols])
                fit = jnp.concatenate([a[:rows] - b[rows:], a[rows:] + b[:rows]], axis=0)
                old = d_raw[:, cols]
            model = m_raw[:, cols]
            new = (model - weight * fit) * inv_alpha - keep * old
            d_raw[:, cols] = new
            vd[:, cols] = new.astype(BF16)
            stats[k, 0:1, :] += lane_sums(new * new)
            stats[k, 3:4, :] += lane_sums(model * model)

        @pl.loop(0, order // wide)
        def _(i):
            cols = pl.ds(pl.multiple_of(i * wide, wide), wide)
            tr = dot_t(vd[...], full[0, cols, :])
            ti = dot_t(vd[...], full[1, cols, :])
            fit = jnp.concatenate([tr[:rows] + ti[rows:], tr[rows:] - ti[:rows]], axis=0)
            new = d_raw[:, cols] - weight * fit
            image[:, cols] = new
            stats[k, 1:2, :] += lane_sums(new * new)
            stats[k, 2:3, :] += lane_sums(new * m_raw[:, cols])

        start_sum(k)
        data_sq, image_sq, cross, model_sq = finish_sum(k)
        old_alpha = alpha
        beta = jnp.sqrt(data_sq)
        alpha = jnp.sqrt(
            image_sq / data_sq
            - 2.0 * cross / old_alpha
            + data_sq * (model_sq / (old_alpha * old_alpha))
        )
        rho = jnp.sqrt(rho_bar * rho_bar + beta * beta)
        cosine, sine = rho_bar / rho, beta / rho
        rho_bar = -cosine * alpha
        step = cosine * phi_bar / rho
        phi_bar = sine * phi_bar
        turn = sine * alpha / rho
        inv_beta, shift = 1.0 / beta, beta / old_alpha
        new_inv = 1.0 / alpha
        old_inv = 1.0 / old_alpha
        last = it == ITERS - 1

        tall = 2 * rows // 4 if rows % 16 == 0 else 2 * rows

        def leave(i, which):
            src, dst = (work, sol_out) if which == 0 else (direc, dir_out)
            per = rows // tall if tall <= rows else 1
            return pltpu.make_async_copy(
                src.at[pl.ds(pl.multiple_of(i * tall, tall), tall), :],
                dst.at[0, lax.div(i, per), pl.ds(pl.multiple_of(lax.rem(i, per) * tall, tall), tall), :],
                out_sem.at[which, i],
            )

        @pl.loop(0, 2 * rows // tall)
        def _(i):
            here = pl.ds(pl.multiple_of(i * tall, tall), tall)

            @pl.loop(0, order // chunk)
            def _(j):
                cols = pl.ds(pl.multiple_of(j * chunk, chunk), chunk)
                model = m_raw[here, cols]
                new = image[here, cols] * inv_beta - shift * model
                if it == 0:
                    old = model * old_inv
                    work[here, cols] = step * old
                else:
                    old = direc[here, cols]
                    work[here, cols] = work[here, cols] + step * old
                direc[here, cols] = new * new_inv - turn * old
                if not last:
                    m_raw[here, cols] = new
                    va[here, cols] = new.astype(BF16)

            if last:
                leave(i, 0).start()
                leave(i, 1).start()

    for k in range(2 + ITERS):
        drain_sum(k)

    @pl.loop(0, m)
    def _(zb):
        for p in range(2):
            settle(zb, p)

    @pl.loop(0, 2 * rows // tall)
    def _(i):
        leave(i, 0).wait()
        leave(i, 1).wait()


def on_device(n, nf, data):
    rows, order = data.shape[2], data.shape[3]
    weight = 1.0 / (3.0 * (2.0 * order) ** 0.5)
    field = pltpu.VMEM((2 * rows, order), F32)
    rounded = pltpu.VMEM((2 * rows, order), BF16)
    rounds = 2 + ITERS
    dma = pltpu.SemaphoreType.DMA
    out = jax.ShapeDtypeStruct(data.shape, F32)
    anywhere = pl.BlockSpec(memory_space=pl.ANY)
    return pl.pallas_call(
        functools.partial(kernel, n, nf, weight),
        out_shape=(out, out),
        in_specs=[anywhere],
        out_specs=(anywhere, anywhere),
        scratch_shapes=[
            pltpu.VMEM((2, order, order), BF16),
            rounded, rounded, field, field, field, field, field,
            pltpu.VMEM((rounds, 8, 128), F32),
            pltpu.VMEM((rounds, n, 8, 128), F32),
            pltpu.VMEM((rounds, 8, 128), F32),
            pltpu.VMEM((rounds, nf, 8, 128), F32),
            dma((4,)), dma((3, n // 2, 2)), dma((n, 2)),
            dma((rounds, n)), dma((rounds, n)),
            dma((rounds, nf)), dma((rounds, nf)),
            dma((2, 4)),
        ],
        compiler_params=pltpu.CompilerParams(
            collective_id=0, has_side_effects=True, vmem_limit_bytes=60 * 2**20
        ),
    )(data)


def solution(mesh):
    spec = P("freq", None, "row", None)
    return jax.shard_map(
        functools.partial(on_device, mesh.shape["row"], mesh.shape["freq"]),
        mesh=mesh,
        in_specs=(spec,),
        out_specs=(spec, spec),
        check_vma=False,
    )
```

time: 448 us -> 217 us (0.48); the launches traced: 440 us -> 217 us
  Pallas kernels: 0 us -> 210 us
  waiting for transfers between devices: 156 us -> 0 us
  blocking collectives: 121 us -> 0 us
  matrix products: 109 us -> 0 us
  other arithmetic: 30.6 us -> 0 us
  between operations: 23.1 us -> 0.65 us
  local copies, waits for them, and re-layouts: 0.1 us -> 6.87 us
    pallas_call x0 -> x1, Pallas kernels: none -> 210 us  [on_device(): pl.pallas_call(functools.partial(kernel, n, nf, weight), out_shape=(out,...]
    all_gather x1 -> x0, waiting for transfers between devices: 156 us -> none  [on_device(): whole = lax.all_gather(data, 'row', axis=2, tiled=True)]
    psum x3 -> x0, blocking collectives: 121 us -> none  [pair_step(): lax.psum((jnp.sum(data_raw * data_raw), jnp.sum(image * image), jnp.sum(i...]
    dot_general x20 -> x0, matrix products: 109 us -> none  [the longest x3 20.7 us: times_adjoint(): jnp.einsum('frk,fnk->frn', rounded[:, 1], block[:, 0], preferred_element_...]
    convert_element_type x4 -> x0, other arithmetic: 13.5 us -> none  [the longest x2 9.89 us: on_device(): model_raw.astype(jnp.bfloat16)]
    sub x1 -> x0, other arithmetic: 8.72 us -> none  [on_device(): direction = model_unit - theta_value / rho_value * direction]
    reduce_sum x3 -> x0, other arithmetic: 8.38 us -> none  [pair_step(): jnp.sum(image * model_unit)]
    unnamed x42 -> x4, local copies, waits for them, and re-layouts: 0.1 us -> 6.87 us
  transfers between devices with their start and end apart: 1 -> 0, of which waited for: 1 -> 0; matrix products, arithmetic and copies ran while one was open for 0% -> 0% of each run, Pallas kernels for 0% -> 0%
where the time goes in v1:
time: 217 us
  Pallas kernels  210 us (97%)
  local copies, waits for them, and re-layouts  6.87 us (3%)
    pallas_call x1, Pallas kernels, on_device(): pl.pallas_call(functools.partial(kernel, n, nf, weight), out_shape=(out,...  210 us
    unnamed x4, local copies, waits for them, and re-layouts  6.87 us

profile of v1, /device:TPU:0, one launch (start us, length us, event | category | flops | bytes accessed | tf_op | source)
XLA Modules:
  0.0 217.2 jit_solution(8621710348042177577)
XLA Ops:
  0.6 209.6 %shard_map.30 = (f32[1,2,256,2048]{3,2,1,0:T(8,128)}, f32[1,2,256,2048]{3,2,1,0:T(8,128)}) custom-call(bf16[1,2,256,2048]{3,2,1,0:T(8,128)(2,1)} %data.1), custom_call_target="tpu_custom_call" | custom-call | tf_op jit(solution)/shard_map/pallas_call | solution.py:368
  210.3 0.0 copy-start
  210.3 4.8 %copy.5 = f32[1,2,256,2048]{3,2,1,0:T(8,128)} copy(f32[1,2,256,2048]{3,2,1,0:T(8,128)} %get-tuple-element.4) | data formatting | bytes 8388608
  215.1 0.0 copy-done
  215.1 2.0 copy.6
Async XLA Ops:
  210.3 4.9 %copy-start = (f32[1,2,256,2048]{3,2,1,0:T(8,128)S(1)}, f32[1,2,256,2048]{3,2,1,0:T(8,128)}, u32[]{:S(2)}) copy-start(f32[1,2,256,2048]{3,2,1,0:T(8,128)} %get-tuple-element.5) | copy-start | bytes 12582916

commit v2 on v1

--- a/solution.py
+++ b/solution.py
@@ -27,10 +27,16 @@
 
 
 def kernel(
-    n, nf, weight, data, sol_out, dir_out,
-    full, va, vd, d_raw, m_raw, image, direc, work, stats, slots, sums, fslots,
-    load_sem, ssem, rsem, st_s, st_r, sf_s, sf_r, out_sem,
+    n, nf, weight, data, *refs,
 ):
+    outs, refs = refs[: ITERS + 1], refs[ITERS + 1 :]
+    coef, refs = refs[0], refs[1:]
+    models, refs = refs[:ITERS], refs[ITERS:]
+    (
+        full, va, vd, d_raw, image, work, stats, slots, sums, fslots,
+        load_sem, ssem, rsem, st_s, st_r, sf_s, sf_r, model_sem, image_sem,
+    ) = refs
+    m_raw = models[0]
     rows, order = data.shape[2], data.shape[3]
     m = n // 2
     me = lax.axis_index("row")
@@ -38,10 +44,29 @@
     z, c = lax.div(me, 2), lax.rem(me, 2)
     overlap = rows % 128 == 0
     unit = rows if overlap else min(order, 256)
-    wide = min(order, 512)
+    wide = min(order // 2, 512)
 
     def at_row(r):
         return {"row": r}
+
+    def halves(body, between):
+        count = order // wide
+        pl.loop(0, count // 2)(body)
+        between()
+        pl.loop(count // 2, count)(body)
+
+    def leave_model(it, p):
+        return pltpu.make_async_copy(
+            models[it].at[pl.ds(p * rows, rows), :], outs[it].at[0, p], model_sem.at[it, p]
+        )
+
+    def leave_image(i, p):
+        cols = pl.ds(pl.multiple_of(i * wide, wide), wide)
+        return pltpu.make_async_copy(
+            image.at[pl.ds(p * rows, rows), cols],
+            outs[ITERS].at[0, p, :, cols],
+            image_sem.at[i, p],
+        )
 
     def piece(zb, cc, p):
         start = pl.multiple_of((zb * 2 + cc) * rows, rows)
@@ -76,12 +101,6 @@
         copy.wait()
 
     stats[...] = jnp.zeros_like(stats)
-
-    @pl.loop(0, order // wide)
-    def _(i):
-        x = vd[:, pl.ds(pl.multiple_of(i * wide, wide), wide)].astype(F32)
-        stats[0, 0:1, :] += lane_sums(x * x)
-
     pl.semaphore_wait(barrier, n - 1 + nf - 1)
 
     def row_stat(k, j):
@@ -115,7 +134,7 @@
         def _(i):
             row_stat(k, lax.rem(me + i, n)).start()
 
-    def finish_sum(k):
+    def middle_sum(k):
         @pl.loop(1, n)
         def _(i):
             row_arrival(k, lax.rem(me + i, n)).wait_recv()
@@ -130,6 +149,7 @@
         def _(i):
             freq_stat(k, lax.rem(mf + i, nf)).start()
 
+    def finish_sum(k):
         @pl.loop(1, nf)
         def _(i):
             freq_arrival(k, lax.rem(mf + i, nf)).wait_recv()
@@ -180,16 +200,22 @@
 
         block_copy(2, zb, c, p, sibling).wait_send()
 
+    spread(z, 0, jnp.bool_(True), jnp.bool_(True))
+
+    @pl.loop(0, order // wide)
+    def _(i):
+        x = vd[:, pl.ds(pl.multiple_of(i * wide, wide), wide)].astype(F32)
+        stats[0, 0:1, :] += lane_sums(x * x)
+
     start_sum(0)
-    yes = m > 0
-    for p in range(2):
-        spread(z, p, jnp.bool_(yes), jnp.bool_(yes))
+    spread(z, 1, jnp.bool_(True), jnp.bool_(True))
 
     @pl.loop(0, order // wide)
     def _(i):
         cols = pl.ds(pl.multiple_of(i * wide, wide), wide)
         work[:, cols] = jnp.zeros((2 * rows, wide), F32)
 
+    middle_sum(0)
     beta = jnp.sqrt(finish_sum(0)[0])
 
     def process(start):
@@ -250,99 +276,99 @@
             process(u * unit)
 
     start_sum(1)
+    for p in range(2):
+        leave_model(0, p).start()
+    middle_sum(1)
     alpha = jnp.sqrt(finish_sum(1)[0])
 
-    chunk = min(order, 256)
     phi_bar, rho_bar = beta, alpha
+    direction, answer = [1.0 / alpha], []
     for it in range(ITERS):
-        k = 2 + it
-        inv_alpha, keep = 1.0 / alpha, alpha / beta
-
-        @pl.loop(0, order // wide)
-        def _(i):
-            cols = pl.ds(pl.multiple_of(i * wide, wide), wide)
-            if it == 0:
-                fit = work[:, cols]
-                old = vd[:, cols].astype(F32)
-            else:
+        last = it == ITERS - 1
+        model_ref = models[it]
+        ka, kb = 2 * it + 1, 2 * it + 2
+
+        if it > 0:
+            def forward(i):
+                cols = pl.ds(pl.multiple_of(i * wide, wide), wide)
                 a = dot(va[...], full[0, :, cols])
                 b = dot(va[...], full[1, :, cols])
-                fit = jnp.concatenate([a[:rows] - b[rows:], a[rows:] + b[:rows]], axis=0)
-                old = d_raw[:, cols]
-            model = m_raw[:, cols]
-            new = (model - weight * fit) * inv_alpha - keep * old
+                work[:, cols] = jnp.concatenate(
+                    [a[:rows] - b[rows:], a[rows:] + b[:rows]], axis=0
+                )
+
+            halves(forward, lambda: middle_sum(ka))
+            alpha = jnp.sqrt(finish_sum(ka)[0])
+            rotate(alpha)
+        inv_alpha, keep = 1.0 / alpha, alpha / beta
+
+        @pl.loop(0, order // wide)
+        def _(i):
+            cols = pl.ds(pl.multiple_of(i * wide, wide), wide)
+            old = vd[:, cols].astype(F32) if it == 0 else d_raw[:, cols]
+            new = (model_ref[:, cols] - weight * work[:, cols]) * inv_alpha - keep * old
             d_raw[:, cols] = new
             vd[:, cols] = new.astype(BF16)
-            stats[k, 0:1, :] += lane_sums(new * new)
-            stats[k, 3:4, :] += lane_sums(model * model)
-
-        @pl.loop(0, order // wide)
-        def _(i):
+            stats[kb, 0:1, :] += lane_sums(new * new)
+
+        start_sum(kb)
+
+        def adjoint(i):
             cols = pl.ds(pl.multiple_of(i * wide, wide), wide)
             tr = dot_t(vd[...], full[0, cols, :])
             ti = dot_t(vd[...], full[1, cols, :])
             fit = jnp.concatenate([tr[:rows] + ti[rows:], tr[rows:] - ti[:rows]], axis=0)
             new = d_raw[:, cols] - weight * fit
             image[:, cols] = new
-            stats[k, 1:2, :] += lane_sums(new * new)
-            stats[k, 2:3, :] += lane_sums(new * m_raw[:, cols])
-
-        start_sum(k)
-        data_sq, image_sq, cross, model_sq = finish_sum(k)
-        old_alpha = alpha
+            if last:
+                stats[kb + 1, 0:1, :] += lane_sums(new * new)
+                stats[kb + 1, 1:2, :] += lane_sums(new * model_ref[:, cols])
+                for p in range(2):
+                    leave_image(i, p).start()
+
+        halves(adjoint, lambda: middle_sum(kb))
+        if last:
+            start_sum(kb + 1)
+        data_sq = finish_sum(kb)[0]
         beta = jnp.sqrt(data_sq)
-        alpha = jnp.sqrt(
-            image_sq / data_sq
-            - 2.0 * cross / old_alpha
-            + data_sq * (model_sq / (old_alpha * old_alpha))
-        )
+        inv_beta, shift = 1.0 / beta, beta / alpha
+
+        if not last:
+            @pl.loop(0, order // wide)
+            def _(i):
+                cols = pl.ds(pl.multiple_of(i * wide, wide), wide)
+                new = image[:, cols] * inv_beta - shift * model_ref[:, cols]
+                models[it + 1][:, cols] = new
+                va[:, cols] = new.astype(BF16)
+                stats[kb + 1, 0:1, :] += lane_sums(new * new)
+
+            start_sum(kb + 1)
+            for p in range(2):
+                leave_model(it + 1, p).start()
+
         rho = jnp.sqrt(rho_bar * rho_bar + beta * beta)
         cosine, sine = rho_bar / rho, beta / rho
-        rho_bar = -cosine * alpha
         step = cosine * phi_bar / rho
         phi_bar = sine * phi_bar
-        turn = sine * alpha / rho
-        inv_beta, shift = 1.0 / beta, beta / old_alpha
-        new_inv = 1.0 / alpha
-        old_inv = 1.0 / old_alpha
-        last = it == ITERS - 1
-
-        tall = 2 * rows // 4 if rows % 16 == 0 else 2 * rows
-
-        def leave(i, which):
-            src, dst = (work, sol_out) if which == 0 else (direc, dir_out)
-            per = rows // tall if tall <= rows else 1
-            return pltpu.make_async_copy(
-                src.at[pl.ds(pl.multiple_of(i * tall, tall), tall), :],
-                dst.at[0, lax.div(i, per), pl.ds(pl.multiple_of(lax.rem(i, per) * tall, tall), tall), :],
-                out_sem.at[which, i],
-            )
-
-        @pl.loop(0, 2 * rows // tall)
-        def _(i):
-            here = pl.ds(pl.multiple_of(i * tall, tall), tall)
-
-            @pl.loop(0, order // chunk)
-            def _(j):
-                cols = pl.ds(pl.multiple_of(j * chunk, chunk), chunk)
-                model = m_raw[here, cols]
-                new = image[here, cols] * inv_beta - shift * model
-                if it == 0:
-                    old = model * old_inv
-                    work[here, cols] = step * old
-                else:
-                    old = direc[here, cols]
-                    work[here, cols] = work[here, cols] + step * old
-                direc[here, cols] = new * new_inv - turn * old
-                if not last:
-                    m_raw[here, cols] = new
-                    va[here, cols] = new.astype(BF16)
-
-            if last:
-                leave(i, 0).start()
-                leave(i, 1).start()
-
-    for k in range(2 + ITERS):
+        answer = [x + step * w for x, w in zip(answer + [0.0], direction)]
+
+        def rotate(alpha, sine=sine, cosine=cosine, rho=rho):
+            nonlocal rho_bar, direction
+            rho_bar = -cosine * alpha
+            turn = sine * alpha / rho
+            direction = [-turn * w for w in direction] + [1.0 / alpha]
+
+    middle_sum(kb + 1)
+    image_sq, cross = finish_sum(kb + 1)[:2]
+    new_alpha = jnp.sqrt(image_sq / data_sq - 2.0 * cross / alpha + data_sq)
+    rotate(new_alpha)
+    tip = direction.pop()
+    direction[-1] = direction[-1] - tip * shift
+    direction.append(tip * inv_beta)
+    for q, value in enumerate(answer + direction):
+        coef[q : q + 1, :] = jnp.broadcast_to(value, (1, 128))
+
+    for k in range(2 + 2 * ITERS):
         drain_sum(k)
 
     @pl.loop(0, m)
@@ -350,10 +376,13 @@
         for p in range(2):
             settle(zb, p)
 
-    @pl.loop(0, 2 * rows // tall)
-    def _(i):
-        leave(i, 0).wait()
-        leave(i, 1).wait()
+    for p in range(2):
+        for it in range(ITERS):
+            leave_model(it, p).wait()
+
+        @pl.loop(0, order // wide)
+        def _(i):
+            leave_image(i, p).wait()
 
 
 def on_device(n, nf, data):
@@ -361,18 +390,19 @@
     weight = 1.0 / (3.0 * (2.0 * order) ** 0.5)
     field = pltpu.VMEM((2 * rows, order), F32)
     rounded = pltpu.VMEM((2 * rows, order), BF16)
-    rounds = 2 + ITERS
+    rounds = 2 + 2 * ITERS
     dma = pltpu.SemaphoreType.DMA
     out = jax.ShapeDtypeStruct(data.shape, F32)
     anywhere = pl.BlockSpec(memory_space=pl.ANY)
-    return pl.pallas_call(
+    *basis, coef = pl.pallas_call(
         functools.partial(kernel, n, nf, weight),
-        out_shape=(out, out),
+        out_shape=(out,) * (ITERS + 1) + (jax.ShapeDtypeStruct((2 * ITERS + 1, 128), F32),),
         in_specs=[anywhere],
-        out_specs=(anywhere, anywhere),
-        scratch_shapes=[
+        out_specs=(anywhere,) * (ITERS + 1) + (pl.BlockSpec(memory_space=pltpu.VMEM),),
+        scratch_shapes=[field] * ITERS
+        + [
             pltpu.VMEM((2, order, order), BF16),
-            rounded, rounded, field, field, field, field, field,
+            rounded, rounded, field, field, field,
             pltpu.VMEM((rounds, 8, 128), F32),
             pltpu.VMEM((rounds, n, 8, 128), F32),
             pltpu.VMEM((rounds, 8, 128), F32),
@@ -380,12 +410,15 @@
             dma((4,)), dma((3, n // 2, 2)), dma((n, 2)),
             dma((rounds, n)), dma((rounds, n)),
             dma((rounds, nf)), dma((rounds, nf)),
-            dma((2, 4)),
+            dma((ITERS, 2)), dma((max(2, order // 512), 2)),
         ],
         compiler_params=pltpu.CompilerParams(
             collective_id=0, has_side_effects=True, vmem_limit_bytes=60 * 2**20
         ),
     )(data)
+    answer = sum(coef[k, 0] * basis[k] for k in range(ITERS))
+    direction = sum(coef[ITERS + k, 0] * basis[k] for k in range(ITERS + 1))
+    return answer, direction
 
 
 def solution(mesh):

time: 217 us -> 215 us (level)
  other arithmetic: 0 us -> 13.6 us
  Pallas kernels: 210 us -> 199 us
  local copies, waits for them, and re-layouts: 6.87 us -> 1.44 us
    add x0 -> x1, other arithmetic: none -> 13.6 us  [on_device(): direction = sum((coef[ITERS + k, 0] * basis[k] for k in range(ITERS + 1)))]
    pallas_call x1, Pallas kernels: 210 us -> 199 us  [on_device(): pl.pallas_call(functools.partial(kernel, n, nf, weight), out_shape=(out,)...]
    unnamed x4 -> x0, local copies, waits for them, and re-layouts: 6.87 us -> none
where the time goes in v2:
time: 215 us
  Pallas kernels  199 us (93%)
  other arithmetic  13.6 us (6%)
    pallas_call x1, Pallas kernels, on_device(): pl.pallas_call(functools.partial(kernel, n, nf, weight), out_shape=(out,)...  199 us
    add x1, other arithmetic, on_device(): direction = sum((coef[ITERS + k, 0] * basis[k] for k in range(ITERS + 1)))  13.6 us

profile of v2, /device:TPU:0, one launch (start us, length us, event | category | flops | bytes accessed | tf_op | source)
XLA Modules:
  0.0 214.9 jit_solution(1667738800422222383)
XLA Ops:
  0.6 199.2 %shard_map.30 = (f32[1,2,256,2048]{3,2,1,0:T(8,128)}, f32[1,2,256,2048]{3,2,1,0:T(8,128)}, f32[1,2,256,2048]{3,2,1,0:T(8,128)}, f32[5,128]{1,0:T(8,128)}) custom-call(bf16[1,2,256,2048]{3,2,1,0:T(8,128)(2,1)} %data.1), custom_call_target="tpu_custom_call" | custom-call | tf_op jit(solution)/shard_map/pallas_call | solution.py:397
  199.9 1.4 fusion
  201.3 13.6 %multiply_add_fusion = (f32[1,2,256,2048]{3,2,1,0:T(8,128)}, f32[1,2,256,2048]{3,2,1,0:T(8,128)}) fusion(f32[1,2,256,2048]{3,2,1,0:T(8,128)} %get-tuple-element.9, f32[1,2,256,2048]{3,2,1,0:T(8,128)} %get-tuple-element.8, f32[1,2,256,2048]{3,2,1,0:T(8,128)} %get-tuple-element.7, f32[]{:T(128)} %bitcast.4, f32[]{:T(128)} %bitcast.3, f32[]{:T(128)} %bitcast.2, ...), kind=kLoop, calls=%fused_computation | loop fusion | flops 8388608 | bytes 20971540 | tf_op jit(solution)/shard_map/add | solution.py:420
